TPU v7x, 32 devices: a whole 2x2x4 slice. The times are simulated.
32 devices in a mesh: replica: 2 (over x), batch: 16 (over z, y, core).
Axes of the slice: x: 2, y: 2, z: 4, core: 2. Of those that a mesh axis runs over, the one named last changes fastest.
Arguments:
- cache_state: bfloat16 [256, 12, 64, 128], P(('replica', 'batch')), parts along dimension 0, may hold values from -6 to 6
- prefill_state: bfloat16 [64, 12, 64, 128], P(('replica', 'batch')), parts along dimension 0, may hold values from -6 to 6
- x_in: bfloat16 [256, 768], P(('replica', 'batch')), parts along dimension 0, may hold values from -6 to 6
- z_in: bfloat16 [256, 768], P(('replica', 'batch')), parts along dimension 0, may hold values from -6 to 6
- b_in: bfloat16 [256, 128], P(('replica', 'batch')), parts along dimension 0, may hold values from -6 to 6
- c_in: bfloat16 [256, 128], P(('replica', 'batch')), parts along dimension 0, may hold values from -0.59765625 to 0.59765625
- dt_in: bfloat16 [256, 12], P(('replica', 'batch')), parts along dimension 0, may hold values from -4 to 4
- dt_bias: float32 [12], replicated, may hold values from -3 to 0.5
- a_log: float32 [12], replicated, may hold values from 0 to 2.5
- d_skip: float32 [12], replicated, may hold values from 0.5 to 1.5
- norm_gain: float32 [768], replicated, may hold values from 0.25 to 1.75
- out_weight: bfloat16 [768, 4096], replicated, may hold values from -0.21875 to 0.21875
- active: int32 [256], P(('replica', 'batch')), parts along dimension 0, may hold values from 0 to 1, as said below
- prefill_count: int32 [32], P(('replica', 'batch')), parts along dimension 0, may hold values from 0 to 2, as said below
- dest_owner: int32 [64], P(('replica', 'batch')), parts along dimension 0, may hold values from 0 to 15, as said below
- dest_slot: int32 [64], P(('replica', 'batch')), parts along dimension 0, may hold values from 0 to 7, as said below
Outputs:
- mixed: bfloat16 [256, 4096], P(('replica', 'batch')), parts along dimension 0
- new_state: bfloat16 [256, 12, 64, 128], P(('replica', 'batch')), parts along dimension 0
There are 2 independent parts, one for each index of `replica`. A program takes and returns all parts, laid end to end along the dimension named above; an argument that names none is the same for every part. Nothing has to cross between parts.
Inputs may be any that keep to these rules, and one draw needn't show every extreme that they name: `active`: at least 2 slots of every device are 0. `prefill_count`: the live rows of a device are its first ones. `dest_owner`: for each row index j below 2, the rows j of the devices go to distinct owners; the two rows of one device go to different owners. So an owner receives at most 2 live rows, at most one from any device, and some owner exactly 2. `dest_slot`: A live row's slot is 0 in the owner's active entries, and no two live rows share an owner and slot.
All inputs are finite; a program needn't handle non-finite values.
Results may differ from a plain program's by a relative error of at most 0.0049.
Values may be sent and summed in bfloat16 or wider, within the bound.
A program may use at most 128 MiB of HBM per device.

v0:
```python
import jax
import jax.numpy as jnp
from jax import lax
from jax.sharding import PartitionSpec as P


def advance(
    state, x_in, z_in, b_in, c_in, dt_in, dt_bias, a_log, d_skip, norm_gain, out_weight, live
):
    rows, heads, hdim, nstate = state.shape
    step = jax.nn.softplus(dt_in.astype(jnp.float32) + dt_bias[None, :])
    decay = jnp.exp(-step * jnp.exp(a_log)[None, :])
    inputs = x_in.astype(jnp.float32).reshape(rows, heads, hdim)
    b_vals = b_in.astype(jnp.float32)
    c_vals = c_in.astype(jnp.float32)
    fresh = (
        state * decay[:, :, None, None]
        + (step[:, :, None] * inputs)[:, :, :, None] * b_vals[:, None, None, :]
    )
    ys = (
        jnp.einsum("rhpn,rn->rhp", fresh, c_vals, precision=lax.Precision.HIGHEST)
        + d_skip[None, :, None] * inputs
    )
    gated = ys.reshape(rows, heads * hdim) * jax.nn.silu(z_in.astype(jnp.float32))
    scale = lax.rsqrt(jnp.mean(gated * gated, axis=1, keepdims=True) + 1e-05)
    normed = jnp.where(live[:, None], gated * scale * norm_gain[None, :], 0.0).astype(jnp.bfloat16)
    mixed = jnp.dot(normed, out_weight, preferred_element_type=jnp.float32).astype(jnp.bfloat16)
    new_state = jnp.where(live[:, None, None, None], fresh, 0.0).astype(jnp.bfloat16)
    return (mixed, new_state)


def body(
    cache_state,
    prefill_state,
    x_in,
    z_in,
    b_in,
    c_in,
    dt_in,
    dt_bias,
    a_log,
    d_skip,
    norm_gain,
    out_weight,
    active,
    prefill_count,
    dest_owner,
    dest_slot,
):
    myself = lax.axis_index("batch")
    slots, heads, hdim, nstate = cache_state.shape
    fresh_rows = prefill_state.shape[0]
    valid = jnp.arange(fresh_rows, dtype=jnp.int32) < prefill_count[0]
    owner_local = jnp.where(valid, dest_owner, -1)
    owner_all, slot_all = (
        lax.all_gather(owner_local, "batch", axis=0, tiled=True),
        lax.all_gather(dest_slot, "batch", axis=0, tiled=True),
    )
    slot_ids = jnp.arange(slots, dtype=jnp.int32)
    onehot = ((owner_all[None, :] == myself) & (slot_all[None, :] == slot_ids[:, None])).astype(
        jnp.bfloat16
    )
    moved = jnp.einsum(
        "sr,rhpn->shpn",
        onehot,
        lax.all_gather(prefill_state, "batch", axis=0, tiled=True),
        preferred_element_type=jnp.float32,
    )
    arrived = jnp.sum(onehot.astype(jnp.float32), axis=1)
    landed = arrived > 0.5
    live = (active > 0) | landed
    state = jnp.where(landed[:, None, None, None], moved, cache_state.astype(jnp.float32))
    return advance(
        state, x_in, z_in, b_in, c_in, dt_in, dt_bias, a_log, d_skip, norm_gain, out_weight, live
    )


def solution(mesh):
    in_specs = (
        P(("replica", "batch"), None, None, None),
        P(("replica", "batch"), None, None, None),
        P(("replica", "batch"), None),
        P(("replica", "batch"), None),
        P(("replica", "batch"), None),
        P(("replica", "batch"), None),
        P(("replica", "batch"), None),
        P(),
        P(),
        P(),
        P(),
        P(),
        P(("replica", "batch")),
        P(("replica", "batch")),
        P(("replica", "batch")),
        P(("replica", "batch")),
    )
    out_specs = (P(("replica", "batch"), None), P(("replica", "batch"), None, None, None))
    return jax.shard_map(body, mesh=mesh, in_specs=in_specs, out_specs=out_specs, check_vma=False)
```

profile of v0, /device:TPU:0, one launch (start us, length us, event | category | flops | bytes accessed | tf_op | source)
XLA Modules:
  0.0 99.9 jit_solution(15233405479906847518)
XLA Ops:
  7.2 0.0 copy-start
  7.2 0.0 all-gather.2.cloned.1.call-start
  7.2 0.7 all-gather.2.cloned.1.call-update
  8.6 0.7 exp.15
  9.2 0.7 convert_element_type.33
  9.9 0.7 multiply_exponential_fusion
  10.6 0.1 copy.31
  10.7 0.8 reshape.45
  11.5 0.1 broadcast_multiply_fusion
  11.6 0.2 copy.32
  11.8 1.2 %dynamic-slice = u32[1]{0:T(128)} dynamic-slice(u32[32]{0:T(128)} %constant.35, u32[]{:T(128)S(6)} %add.37), dynamic_slice_sizes={1} | dynamic-slice | bytes 12
  13.7 0.9 dynamic-update-slice.1
  14.6 0.7 fusion.21
  15.3 13.8 %all-reduce.2 = (s32[32]{0:T(128)S(1)}, s32[32]{0:T(128)S(1)}) all-reduce(s32[32]{0:T(128)S(1)} %dynamic-update-slice.1, s32[32]{0:T(128)S(1)} %fusion.21), channel_id=1, replica_groups=mesh['replica'=2,'batch'=16] {'batch'}, use_global_device_ids=true, to_apply=%add.1 | all-reduce | flops 64 | bytes 512
  29.1 0.1 convert_reduce_fusion
  29.3 0.7 compare_or_fusion
  29.9 44.6 %all-gather.2.cloned.1.call-done = bf16[32,12,64,128]{3,2,1,0:T(8,128)(2,1)} async-done(((bf16[2,12,64,128]{3,2,1,0:T(8,128)(2,1)}), bf16[32,12,64,128]{3,2,1,0:T(8,128)(2,1)}) %all-gather.2.cloned.1.call-update) | async-done | bytes 6291472 | tf_op jit(solution)/shard_map/all_gather | solution.py:66
  74.5 8.4 %select_convert_fusion = (bf16[8,12,64,128]{3,0,2,1:T(8,128)(2,1)S(1)}, f32[8,12,64,128]{3,0,2,1:T(8,128)S(1)}) fusion(pred[8]{0:T(512)(128)(4,1)S(1)} %get-tuple-element.12, f32[8,128]{1,0:T(8,128)S(1)} %convert_element_type.33, f32[8,12,64]{0,2,1:T(8,128)S(1)} %copy.32, f32[8,12]{0,1:T(8,128)S(1)} %copy.31, bf16[8,12,64,128]{3,2,1,0:T(8,128)(2,1)} %param.16, ...), kind=kOutput, calls=%fused_computation.5 | convolution fusion | flops 55050752 | bytes 12612144 | tf_op jit(solution)/shard_map/sr,rhpn->shpn/dot_general | solution.py:63
  83.0 1.6 %copy.33 = bf16[8,12,64,128]{3,2,1,0:T(8,128)(2,1)} copy(bf16[8,12,64,128]{3,0,2,1:T(8,128)(2,1)S(1)} %get-tuple-element.14) | data formatting | bytes 3145728
  84.6 3.8 %fusion.2 = f32[8,1,12,64]{3,1,2,0:T(1,128)S(1)} fusion(f32[8,12,64,128]{3,0,2,1:T(8,128)S(1)} %get-tuple-element.15, bf16[8,128,1,1]{1,0,2,3:T(8,128)(2,1)S(1)} %bitcast.14), kind=kOutput, calls=%fused_computation.3 | convolution fusion | flops 9437184 | bytes 3172352 | tf_op jit(solution)/shard_map/rhpn,rn->rhp/dot_general | solution.py:21
  88.3 0.1 bitcast_add_fusion
  88.4 0.1 reshape.43
  88.5 0.1 multiply_reduce_fusion
  88.7 4.4 %convolution_convert_fusion = bf16[8,4096]{1,0:T(8,128)(2,1)} fusion(bf16[768,4096]{1,0:T(8,128)(2,1)} %param.27, f32[768]{0:T(1024)S(1)} %copy-done.2, f32[8]{0:T(128)S(1)} %add_rsqrt_fusion, pred[8]{0:T(512)(128)(4,1)S(1)} %get-tuple-element.12, f32[8,768]{1,0:T(8,128)S(1)} %reshape.43, bf16[8,768]{1,0:T(8,128)(2,1)S(1)} %copy-done.1), kind=kOutput, calls=%fused_computation.2 | convolution fusion | flops 50425856 | bytes 6396968 | tf_op jit(solution)/shard_map/dot_general | solution.py:27
  (11 shorter events, 0.0 us)
Async XLA Ops:
  7.2 77.4 %copy-start = (bf16[8,128]{1,0:T(8,128)(2,1)S(1)}, bf16[8,128]{1,0:T(8,128)(2,1)}, u32[]{:S(2)}) copy-start(bf16[8,128]{1,0:T(8,128)(2,1)} %param.21) | copy-start | bytes 6148
  7.2 67.3 %all-gather.2.cloned.1.call-start = ((), (), s32[]{:S(2)}) async-start(), calls=%async_computation | async-start | bytes 6684672 | tf_op jit(solution)/shard_map/all_gather | solution.py:66
  83.0 5.4 %copy-start.3 = (f32[12]{0:T(128)S(1)}, f32[12]{0:T(128)}, u32[]{:S(2)}) copy-start(f32[12]{0:T(128)} %param.25) | copy-start | bytes 148
  83.0 5.5 %copy-start.1 = (bf16[8,768]{1,0:T(8,128)(2,1)S(1)}, bf16[8,768]{1,0:T(8,128)(2,1)}, u32[]{:S(2)}) copy-start(bf16[8,768]{1,0:T(8,128)(2,1)} %param.19) | copy-start | bytes 36868
  83.0 5.7 %copy-start.2 = (f32[768]{0:T(1024)S(1)}, f32[768]{0:T(1024)}, u32[]{:S(2)}) copy-start(f32[768]{0:T(1024)} %param.26) | copy-start | bytes 9220
Sparse Core Ops, SparseCore 0:
  10.3 64.2 all-gather.1
where the time goes:
time: 100 us; the launch traced here: 99.9 us
  waiting for transfers between devices  45.3 us (45%)
  matrix products  16.6 us (17%)
  between operations  15.4 us (15%)
  blocking collectives  13.8 us (14%)
  local copies, waits for them, and re-layouts  5.49 us (5%)
  other arithmetic  3.25 us (3%)
    all_gather x1, waiting for transfers between devices, body(): lax.all_gather(prefill_state, 'batch', axis=0, tiled=True)  44.6 us
    unnamed x1, blocking collectives  13.8 us
    dot_general x1, matrix products, body(): jnp.einsum('sr,rhpn->shpn', onehot, lax.all_gather(prefill_state, 'batch'...  8.45 us
    dot_general x1, matrix products, advance(): jnp.dot(normed, out_weight, preferred_element_type=jnp.float32)  4.39 us
    dot_general x1, matrix products, advance(): jnp.einsum('rhpn,rn->rhp', fresh, c_vals, precision=lax.Precision.HIGHEST)  3.76 us
    unnamed x13, local copies, waits for them, and re-layouts  3.69 us
  transfers between devices with their start and end apart: 1, of which 1 were waited for; matrix products, arithmetic and copies ran while one was open for 7% of the time, Pallas kernels for 0%

commit v1 on v0

--- a/solution.py
+++ b/solution.py
@@ -63,7 +63,15 @@
     moved = jnp.einsum(
         "sr,rhpn->shpn",
         onehot,
-        lax.all_gather(prefill_state, "batch", axis=0, tiled=True),
+        jnp.concatenate(
+            lax.all_to_all(
+                jnp.stack([prefill_state for _ in range(lax.axis_size("batch"))], axis=0),
+                "batch",
+                0,
+                0,
+            ),
+            axis=0,
+        ),
         preferred_element_type=jnp.float32,
     )
     arrived = jnp.sum(onehot.astype(jnp.float32), axis=1)

time: 100 us -> 174 us (1.74)
  blocking collectives: 13.8 us -> 136 us
  waiting for transfers between devices: 45.3 us -> 0.01 us
  between operations: 15.4 us -> 2.22 us
  local copies, waits for them, and re-layouts: 5.49 us -> 15.9 us
  starting transfers between devices: 0.04 us -> 7.6 us
  matrix products: 16.6 us -> 10.6 us
  other arithmetic: 3.25 us -> 1.12 us
    unnamed x1, blocking collectives: 13.8 us -> 136 us
    all_gather x1 -> x0, waiting for transfers between devices: 44.6 us -> none  [body(): lax.all_gather(prefill_state, 'batch', axis=0, tiled=True)]
    all_to_all x0 -> x1, starting transfers between devices: none -> 7.6 us  [body(): lax.all_to_all(jnp.stack([prefill_state for _ in range(lax.axis_size('bat...]
    dot_general x1, matrix products: 8.45 us -> 2.48 us  [body(): jnp.einsum('sr,rhpn->shpn', onehot, jnp.concatenate(lax.all_to_all(jnp.st...]
    another operation x0 -> x1, local copies, waits for them, and re-layouts: none -> 5.82 us  [body(): jnp.stack([prefill_state for _ in range(lax.axis_size('batch'))], axis=0)]
    all_to_all x0 -> x1, local copies, waits for them, and re-layouts: none -> 5.77 us  [body(): lax.all_to_all(jnp.stack([prefill_state for _ in range(lax.axis_size('bat...]
    unnamed x13 -> x48, local copies, waits for them, and re-layouts: 3.69 us -> 3.93 us
  transfers between devices with their start and end apart: 1 -> 1, of which waited for: 1 -> 0; matrix products, arithmetic and copies ran while one was open for 7% -> 1% of each run, Pallas kernels for 0% -> 0%
where the time goes in v1:
time: 174 us
  blocking collectives  136 us (78%)
  local copies, waits for them, and re-layouts  15.9 us (9%)
  matrix products  10.6 us (6%)
  starting transfers between devices  7.6 us (4%)
  between operations  2.22 us (1%)
    unnamed x1, blocking collectives  136 us
    all_to_all x1, starting transfers between devices, body(): lax.all_to_all(jnp.stack([prefill_state for _ in range(lax.axis_size('bat...  7.6 us
    another operation x1, local copies, waits for them, and re-layouts, body(): jnp.stack([prefill_state for _ in range(lax.axis_size('batch'))], axis=0)  5.82 us
    all_to_all x1, local copies, waits for them, and re-layouts, body(): lax.all_to_all(jnp.stack([prefill_state for _ in range(lax.axis_size('bat...  5.77 us
    dot_general x1, matrix products, advance(): jnp.dot(normed, out_weight, preferred_element_type=jnp.float32)  4.38 us
    unnamed x48, local copies, waits for them, and re-layouts  3.93 us
    dot_general x1, matrix products, advance(): jnp.einsum('rhpn,rn->rhp', fresh, c_vals, precision=lax.Precision.HIGHEST)  3.76 us
  transfers between devices with their start and end apart: 1, of which 0 were waited for; matrix products, arithmetic and copies ran while one was open for 1% of the time, Pallas kernels for 0%

profile of v1, /device:TPU:0, one launch (start us, length us, event | category | flops | bytes accessed | tf_op | source)
XLA Modules:
  0.0 173.8 jit_solution(13123821720947897466)
XLA Ops:
  0.6 0.0 copy-start
  0.6 1.4 copy.29
  2.1 5.8 %stack.2 = bf16[16,2,12,64,128]{4,1,3,2,0:T(2,128)(2,1)} broadcast(bf16[2,12,64,128]{3,0,2,1:T(2,128)(2,1)S(1)} %copy.29), dimensions={1,2,3,4} | broadcast | bytes 6684672 | tf_op jit(solution)/shard_map/stack | solution.py:68
  7.9 0.0 copy-start.20
  8.0 7.6 %all-to-all-start = ((bf16[16,2,12,64,128]{4,1,3,2,0:T(2,128)(2,1)}), bf16[16,2,12,64,128]{4,1,3,2,0:T(2,128)(2,1)}, u32[]{:S(2)}, u32[]{:S(2)}) async-start(bf16[16,2,12,64,128]{4,1,3,2,0:T(2,128)(2,1)} %stack.2), calls=%async_computation | async-start | bytes 12582912 | tf_op jit(solution)/shard_map/all_to_all | solution.py:67
  16.2 0.1 reshape.51
  16.4 0.1 broadcast_multiply_fusion
  16.5 0.2 copy.33
  16.7 0.1 copy.32
  16.7 0.6 dynamic-slice
  18.0 0.2 dynamic-update-slice.1
  18.3 0.1 fusion.17
  18.3 136.3 %all-reduce.2 = (s32[32]{0:T(128)S(1)}, s32[32]{0:T(128)S(1)}) all-reduce(s32[32]{0:T(128)S(1)} %dynamic-update-slice.1, s32[32]{0:T(128)S(1)} %fusion.17), channel_id=1, replica_groups=mesh['replica'=2,'batch'=16] {'batch'}, use_global_device_ids=true, to_apply=%add.1 | all-reduce | flops 64 | bytes 512
  154.7 0.1 convert_reduce_fusion
  154.8 0.6 compare_or_fusion
  155.4 5.8 %copy.30 = bf16[16,2,12,64,128]{4,1,0,3,2:T(2,128)(2,1)S(1)} copy(bf16[16,2,12,64,128]{4,1,3,2,0:T(2,128)(2,1)} %all-to-all-done) | data formatting | bytes 12582912 | tf_op jit(solution)/shard_map/all_to_all | solution.py:67
  161.2 2.5 %select_convert_fusion = (bf16[8,12,64,128]{3,0,2,1:T(8,128)(2,1)S(1)}, f32[8,12,64,128]{3,0,2,1:T(8,128)S(1)}) fusion(pred[8]{0:T(512)(128)(4,1)S(1)} %copy-done.6, f32[8,128]{1,0:T(8,128)S(1)} %convert_element_type.33, f32[8,12,64]{0,2,1:T(8,128)S(1)} %copy.33, f32[8,12]{0,1:T(8,128)S(1)} %copy.32, bf16[8,12,64,128]{3,2,1,0:T(8,128)(2,1)S(1)} %copy-done.1, ...), kind=kOutput, calls=%fused_computation.3 | convolution fusion | flops 55050752 | bytes 12612144 | tf_op jit(solution)/shard_map/sr,rhpn->shpn/dot_general | solution.py:63
  163.8 3.8 %fusion = f32[8,1,12,64]{3,1,2,0:T(1,128)S(1)} fusion(f32[8,12,64,128]{3,0,2,1:T(8,128)S(1)} %get-tuple-element.15, bf16[8,128,1,1]{1,0,2,3:T(8,128)(2,1)S(1)} %bitcast.16), kind=kOutput, calls=%fused_computation.1 | convolution fusion | flops 9437184 | bytes 3172352 | tf_op jit(solution)/shard_map/rhpn,rn->rhp/dot_general | solution.py:21
  167.5 0.0 copy-done.12
  167.6 0.1 bitcast_add_fusion
  167.6 0.1 reshape.49
  167.7 0.1 multiply_reduce_fusion
  167.9 1.6 copy.34
  169.4 4.4 %convolution_convert_fusion = bf16[8,4096]{1,0:T(8,128)(2,1)} fusion(bf16[768,4096]{1,0:T(8,128)(2,1)} %param.27, f32[768]{0:T(1024)S(1)} %copy-done.8, f32[8]{0:T(128)S(1)} %add_rsqrt_fusion, pred[8]{0:T(512)(128)(4,1)S(1)} %copy-done.7, f32[8,768]{1,0:T(8,128)S(1)} %reshape.49, bf16[8,768]{1,0:T(8,128)(2,1)S(1)} %copy-done.4), kind=kOutput, calls=%fused_computation | convolution fusion | flops 50425856 | bytes 6396968 | tf_op jit(solution)/shard_map/dot_general | solution.py:27
  (47 shorter events, 0.1 us)
Async XLA Ops:
  0.6 163.1 %copy-start = (bf16[8,128]{1,0:T(8,128)(2,1)S(1)}, bf16[8,128]{1,0:T(8,128)(2,1)}, u32[]{:S(2)}) copy-start(bf16[8,128]{1,0:T(8,128)(2,1)} %param.21) | copy-start | bytes 6148
  7.9 8.3 %copy-start.5 = (bf16[8,768]{1,0:T(8,128)(2,1)S(1)}, bf16[8,768]{1,0:T(8,128)(2,1)}, u32[]{:S(2)}) copy-start(bf16[8,768]{1,0:T(8,128)(2,1)} %param.18) | copy-start | bytes 36868
  7.9 8.4 %copy-start.18 = (f32[12]{0:T(128)S(1)}, f32[12]{0:T(128)}, u32[]{:S(2)}) copy-start(f32[12]{0:T(128)} %param.24) | copy-start | bytes 148
  7.9 8.5 %copy-start.11 = (bf16[8,12]{1,0:T(8,128)(2,1)S(1)}, bf16[8,12]{1,0:T(8,128)(2,1)}, u32[]{:S(2)}) copy-start(bf16[8,12]{1,0:T(8,128)(2,1)} %param.22) | copy-start | bytes 580
  7.9 8.5 %copy-start.15 = (f32[12]{0:T(128)S(1)}, f32[12]{0:T(128)}, u32[]{:S(2)}) copy-start(f32[12]{0:T(128)} %param.23) | copy-start | bytes 148
  7.9 8.8 %copy-start.10 = (bf16[8,128]{1,0:T(8,128)(2,1)S(1)}, bf16[8,128]{1,0:T(8,128)(2,1)}, u32[]{:S(2)}) copy-start(bf16[8,128]{1,0:T(8,128)(2,1)} %param.20) | copy-start | bytes 6148
  7.9 8.8 %copy-start.20 = (u32[32]{0:T(128)S(1)}, u32[32]{0:T(128)}, u32[]{:S(2)}) copy-start(u32[32]{0:T(128)} %constant.35) | copy-start | bytes 388
  7.9 10.1 %copy-start.19 = (s32[2]{0:T(128)S(1)}, s32[2]{0:T(128)}, u32[]{:S(2)}) copy-start(s32[2]{0:T(128)} %param.31) | copy-start | bytes 28
  7.9 10.3 %copy-start.16 = (s32[2]{0:T(128)S(1)}, s32[2]{0:T(128)}, u32[]{:S(2)}) copy-start(s32[2]{0:T(128)} %param.30) | copy-start | bytes 28
  7.9 146.9 %copy-start.17 = (s32[8]{0:T(128)S(1)}, s32[8]{0:T(128)}, u32[]{:S(2)}) copy-start(s32[8]{0:T(128)} %param.28) | copy-start | bytes 100
  8.0 147.4 %all-to-all-start = ((bf16[16,2,12,64,128]{4,1,3,2,0:T(2,128)(2,1)}), bf16[16,2,12,64,128]{4,1,3,2,0:T(2,128)(2,1)}, u32[]{:S(2)}, u32[]{:S(2)}) async-start(bf16[16,2,12,64,128]{4,1,3,2,0:T(2,128)(2,1)} %stack.2), calls=%async_computation | async-start | bytes 12582912 | tf_op jit(solution)/shard_map/all_to_all | solution.py:67
  16.3 144.9 %copy-start.2 = (f32[8,12,64]{2,1,0:T(8,128)}, f32[8,12,64]{2,1,0:T(8,128)S(1)}, u32[]{:S(2)}) copy-start(f32[8,12,64]{2,1,0:T(8,128)S(1)} %reshape.51) | copy-start | bytes 73732
  154.7 6.5 %copy-start.13 = (s32[32]{0:T(128)}, s32[32]{0:T(128)S(1)}, u32[]{:S(2)}) copy-start(s32[32]{0:T(128)S(1)} %get-tuple-element.8) | copy-start | bytes 388
  154.7 6.5 %copy-start.14 = (pred[32]{0:T(512)(128)(4,1)}, pred[32]{0:T(512)(128)(4,1)S(1)}, u32[]{:S(2)}) copy-start(pred[32]{0:T(512)(128)(4,1)S(1)} %broadcast_compare_fusion.1) | copy-start | bytes 100
  155.4 5.8 %copy-start.1 = (bf16[8,12,64,128]{3,2,1,0:T(8,128)(2,1)S(1)}, bf16[8,12,64,128]{3,2,1,0:T(8,128)(2,1)}, u32[]{:S(2)}) copy-start(bf16[8,12,64,128]{3,2,1,0:T(8,128)(2,1)} %param.16) | copy-start | bytes 4718596
  155.4 5.8 %copy-start.6 = (pred[8]{0:T(512)(128)(4,1)S(1)}, pred[8]{0:T(512)(128)(4,1)}, u32[]{:S(2)}) copy-start(pred[8]{0:T(512)(128)(4,1)} %get-tuple-element.12) | copy-start | bytes 28
  155.4 5.8 %copy-start.9 = (pred[8]{0:T(512)(128)(4,1)S(1)}, pred[8]{0:T(512)(128)(4,1)}, u32[]{:S(2)}) copy-start(pred[8]{0:T(512)(128)(4,1)} %get-tuple-element.13) | copy-start | bytes 28
  163.7 3.8 %copy-start.3 = (f32[8,12,64]{2,1,0:T(8,128)S(1)}, f32[8,12,64]{2,1,0:T(8,128)}, u32[]{:S(2)}) copy-start(f32[8,12,64]{2,1,0:T(8,128)} %copy-done.2) | copy-start | bytes 73732
  163.7 3.8 %copy-start.12 = (f32[12]{0:T(128)S(1)}, f32[12]{0:T(128)}, u32[]{:S(2)}) copy-start(f32[12]{0:T(128)} %param.25) | copy-start | bytes 148
  163.7 4.0 %copy-start.4 = (bf16[8,768]{1,0:T(8,128)(2,1)S(1)}, bf16[8,768]{1,0:T(8,128)(2,1)}, u32[]{:S(2)}) copy-start(bf16[8,768]{1,0:T(8,128)(2,1)} %param.19) | copy-start | bytes 36868
  163.8 5.7 %copy-start.7 = (pred[8]{0:T(512)(128)(4,1)S(1)}, pred[8]{0:T(512)(128)(4,1)}, u32[]{:S(2)}) copy-start(pred[8]{0:T(512)(128)(4,1)} %get-tuple-element.12) | copy-start | bytes 28
  163.8 5.7 %copy-start.8 = (f32[768]{0:T(1024)S(1)}, f32[768]{0:T(1024)}, u32[]{:S(2)}) copy-start(f32[768]{0:T(1024)} %param.26) | copy-start | bytes 9220
